TPU v7x, 32 devices: a whole 2x2x4 slice. The times are simulated.
32 devices in a mesh: row: 8 (over y, x, core), col: 4 (over z).
Axes of the slice: x: 2, y: 2, z: 4, core: 2. Of those that a mesh axis runs over, the one named last changes fastest.
Arguments:
- pair_factors: float32 [12288, 1024], P(('row', 'col')), may hold values from -0.09375 to 0.09375
- k_prev: float32 [12288, 12288], P('row', 'col'), as said below
- energies: float32 [12288], P('row'), may hold values from 0.3 to 2
Outputs:
- casida: float32 [12288, 12288], P('row', 'col')
- vectors: float32 [12288, 8], P('row')
- images: float32 [12288, 8], P('row')
- tridiagonal: float32 [2, 8], replicated
Inputs may be any that keep to these rules, and one draw needn't show every extreme that they name: k_prev is exactly symmetric.
All inputs are finite; a program needn't handle non-finite values.
Results may differ from a plain program's by a relative error of at most 0.0003.
Values sent between devices are 32-bit elements; how exact they have to be, the bound alone decides.
No kernel may reach another device: no remote copies, remote signals or barrier semaphores. Data moves between devices by JAX's collectives and lax.ppermute only.
A program may use at most 128 MiB of HBM per device.

v0:
```python
import jax
import jax.numpy as jnp
from jax import lax
from jax.sharding import PartitionSpec as P

N = 12288
PANEL_W = 512
PC = 8


def from_root(value, axis, root):
    mine = lax.axis_index(axis) == root
    return lax.psum(jnp.where(mine, value, jnp.zeros_like(value)), axis)


def shards(pair_factors, k_prev, energies):
    rows_here, cols_here = k_prev.shape
    per_col = lax.axis_size("row") // lax.axis_size("col")
    row_index = lax.axis_index("row")
    col_index = lax.axis_index("col")
    total = jnp.zeros((rows_here, cols_here), jnp.float32)
    aux_here = pair_factors.shape[1]
    width = PANEL_W
    for start_at in range(0, aux_here, width):
        stop_at = min(start_at + width, aux_here)
        piece = pair_factors[:, start_at:stop_at]
        left_rows = lax.all_gather(piece, "col", axis=0, tiled=True)
        right_parts = []
        for offset in range(per_col):
            right_parts.append(from_root(left_rows, "row", per_col * col_index + offset))
        right_rows = jnp.concatenate(right_parts, axis=0)
        total = total + lax.dot_general(
            left_rows,
            right_rows,
            (((1,), (1,)), ((), ())),
            precision=lax.Precision.HIGHEST,
            preferred_element_type=jnp.float32,
        )
    global_rows = row_index * rows_here + jnp.arange(rows_here, dtype=jnp.int32)
    global_cols = col_index * cols_here + jnp.arange(cols_here, dtype=jnp.int32)
    on_diagonal = global_rows[:, None] == global_cols[None, :]
    casida = 4.0 * (k_prev + total) + jnp.where(on_diagonal, energies[:, None], 0.0)
    col_ids = jnp.arange(PC, dtype=jnp.int32)
    scale = jnp.sqrt(jnp.float32(N))
    diag_list = []
    sub_list = []
    spread = from_root(casida[:, :PC], "col", 0)
    panel = lax.all_gather(spread, "row", axis=0, tiled=True)
    total_rows = panel.shape[0]
    all_rows = jnp.arange(total_rows, dtype=jnp.int32)
    upper_full = jnp.zeros((total_rows, PC), jnp.float32)
    lower_full = jnp.zeros((total_rows, PC), jnp.float32)
    for column_at in range(PC):
        column = (
            panel[:, column_at]
            - jnp.dot(upper_full, lower_full[column_at], precision=lax.Precision.HIGHEST)
            - jnp.dot(lower_full, upper_full[column_at], precision=lax.Precision.HIGHEST)
        )
        diag_list.append(column[column_at])
        below = jnp.where(all_rows > column_at, column, 0.0)
        lead = column[column_at + 1]
        sigma = jnp.sum(below * below)
        root = jnp.sqrt(sigma)
        alpha = jnp.where(lead >= 0, -root, root)
        length = jnp.sqrt(jnp.maximum(2.0 * (sigma + jnp.abs(lead) * root), 1.0))
        unit = (below - alpha * (all_rows == column_at + 1).astype(jnp.float32)) / length
        unit_cols = lax.dynamic_slice_in_dim(unit, col_index * cols_here, cols_here, 0)
        partial_rows = jnp.dot(casida, unit_cols, precision=lax.Precision.HIGHEST)
        placed = lax.dynamic_update_slice_in_dim(
            jnp.zeros((total_rows,), jnp.float32), partial_rows, row_index * rows_here, 0
        )
        image = lax.psum(placed, ("row", "col"))
        image = image - jnp.dot(
            upper_full,
            jnp.dot(lower_full.T, unit, precision=lax.Precision.HIGHEST),
            precision=lax.Precision.HIGHEST,
        )
        image = image - jnp.dot(
            lower_full,
            jnp.dot(upper_full.T, unit, precision=lax.Precision.HIGHEST),
            precision=lax.Precision.HIGHEST,
        )
        image = 2.0 * image
        partner = image - jnp.sum(image * unit) * unit
        pick = (col_ids == column_at).astype(jnp.float32)[None, :]
        upper_full = upper_full + unit[:, None] * pick
        lower_full = lower_full + partner[:, None] * pick
        sub_list.append(alpha)
    upper = lax.dynamic_slice_in_dim(upper_full, row_index * rows_here, rows_here, 0)
    lower = lax.dynamic_slice_in_dim(lower_full, row_index * rows_here, rows_here, 0)
    tridiagonal = jnp.stack([jnp.stack(diag_list), jnp.stack(sub_list)])
    return (casida, scale * upper, scale * lower, tridiagonal)


def solution(mesh):
    in_specs = (P(("row", "col"), None), P("row", "col"), P("row"))
    out_specs = (P("row", "col"), P("row", None), P("row", None), P())
    return jax.shard_map(shards, mesh=mesh, in_specs=in_specs, out_specs=out_specs, check_vma=False)
```

profile of v0, /device:TPU:0, one launch (start us, length us, event | category | flops | bytes accessed | tf_op | source)
XLA Modules:
  0.0 965.6 jit_solution(18281307544850483089)
XLA Ops:
  7.2 2.6 fusion.234
  9.9 0.7 all-gather.3.cloned.1.call-update
  10.7 65.6 %all-gather.5.cloned.1.call-done = f32[1536,512]{1,0:T(8,128)} async-done(((f32[384,512]{1,0:T(8,128)}), f32[1536,512]{1,0:T(8,128)}) %all-gather.5.cloned.1.call-update) | async-done | bytes 3145744 | tf_op jit(solution)/shard_map/all_gather | solution.py:27
  76.3 5.6 broadcast_select_fusion.1
  81.9 58.1 %all-gather.3.cloned.1.call-done = f32[1536,512]{1,0:T(8,128)} async-done(((f32[384,512]{1,0:T(8,128)}), f32[1536,512]{1,0:T(8,128)}) %all-gather.3.cloned.1.call-update) | async-done | bytes 3145744 | tf_op jit(solution)/shard_map/all_gather | solution.py:27
  140.0 5.6 broadcast_select_fusion.3
  145.6 0.7 broadcast_reduce_fusion
  146.3 18.8 %copy.9 = f32[1536,3072]{0,1:T(8,128)} copy(f32[1536,3072]{1,0:T(8,128)} %param.4) | data formatting | bytes 37748736 | tf_op args[1]
  165.1 151.2 %all-reduce.3.cloned.1.call-done = (f32[1536,512]{1,0:T(8,128)}, f32[1536,512]{1,0:T(8,128)}, f32[1536,512]{1,0:T(8,128)}, f32[1536,512]{1,0:T(8,128)}) async-done(((f32[1536,512]{1,0:T(8,128)}, f32[1536,512]{1,0:T(8,128)}, f32[1536,512]{1,0:T(8,128)}, f32[1536,512]{1,0:T(8,128)}), (f32[1536,512]{1,0:T(8,128)}, f32[1536,512]{1,0:T(8,128)}, f32[1536,512]{1,0:T(8,128)}, ...) | async-done | bytes 12582928 | tf_op jit(solution)/shard_map/psum | solution.py:13
  316.4 34.6 %fusion.2 = f32[3072,1536]{1,0:T(8,128)} fusion(f32[1536,512]{1,0:T(8,128)S(1)} %copy-done.1, f32[1536,512]{1,0:T(8,128)} %get-tuple-element.12, f32[1536,512]{1,0:T(8,128)} %get-tuple-element.13), kind=kOutput, calls=%fused_computation.3 | convolution fusion | flops 28992602112 | bytes 28311552 | tf_op jit(solution)/shard_map/dot_general | solution.py:32
  351.0 39.2 %fusion.1 = f32[1536,3072]{0,1:T(8,128)S(1)} fusion(f32[1536,3072]{0,1:T(8,128)} %copy.9, f32[3072,1536]{1,0:T(8,128)} %fusion.2, f32[1536,512]{1,0:T(8,128)} %all-gather.5.cloned.1.call-done, f32[1536]{0:T(1024)S(1)} %copy-done.2, s32[1536]{0:T(1024)S(1)} %iota_add_fusion.1, s32[3072]{0:T(1024)S(1)} %iota_add_fusion, f32[1536,512]{1,0:T(8,128)} %get-tuple-element.14, ...), kind=kOutput, calls=%fused_computation.2 | convolution fusion | flops 29020913664 | bytes 66084864 | tf_op jit(solution)/shard_map/dot_general | solution.py:32
  390.2 6.5 copy-done
  396.7 19.5 %psum.95 = f32[1536,8]{0,1:T(8,128)S(1)} all-reduce(f32[1536,8]{0,1:T(8,128)S(1)} %slice_select_fusion), channel_id=1, replica_groups=mesh['row'=8,'col'=4] {'col'}, use_global_device_ids=true, to_apply=%region_4.5 | all-reduce | flops 12288 | bytes 98304 | tf_op jit(solution)/shard_map/psum | solution.py:13
  416.2 9.5 all_gather.11
  426.0 0.7 broadcast.265
  430.6 12.9 %convolution_reduce_fusion.7 = f32[1536]{0:T(1024)S(1)} fusion(f32[1536,3072]{0,1:T(8,128)} %copy-done, f32[3072,1]{0,1:T(1,128)S(1)} %bitcast.304), kind=kOutput, calls=%fused_computation.21 | convolution fusion | flops 56623104 | bytes 18892800 | tf_op jit(solution)/shard_map/dot_general | solution.py:68
  443.8 38.0 %psum.96 = f32[12288]{0:T(1024)S(1)} all-reduce(f32[12288]{0:T(1024)S(1)} %dynamic_update_slice.24), channel_id=1, replica_groups=mesh['row'=8,'col'=4] {'row','col'}, use_global_device_ids=true, to_apply=%region_6.7 | all-reduce | flops 12288 | bytes 98304 | tf_op jit(solution)/shard_map/psum | solution.py:72
  481.8 1.6 fusion.12
  483.4 0.7 broadcast.267
  484.7 0.7 multiply_subtract_fusion.7
  490.8 1.0 convolution_bitcast_fusion.13
  491.8 1.0 convolution_bitcast_fusion.12
  493.4 12.9 %convolution_reduce_fusion.6 = f32[1536]{0:T(1024)S(1)} fusion(f32[1536,3072]{0,1:T(8,128)} %copy-done, f32[3072,1]{0,1:T(1,128)S(1)} %bitcast.298), kind=kOutput, calls=%fused_computation.20 | convolution fusion | flops 56623104 | bytes 18892800 | tf_op jit(solution)/shard_map/dot_general | solution.py:68
  506.6 41.5 %psum.97 = f32[12288]{0:T(1024)S(1)} all-reduce(f32[12288]{0:T(1024)S(1)} %dynamic_update_slice.25), channel_id=1, replica_groups=mesh['row'=8,'col'=4] {'row','col'}, use_global_device_ids=true, to_apply=%region_9.10 | all-reduce | flops 12288 | bytes 98304 | tf_op jit(solution)/shard_map/psum | solution.py:72
  549.3 0.7 multiply_subtract_fusion.6
  555.5 1.0 convolution_bitcast_fusion.11
  556.5 1.0 convolution_bitcast_fusion.10
  558.1 12.9 %convolution_reduce_fusion.5 = f32[1536]{0:T(1024)S(1)} fusion(f32[1536,3072]{0,1:T(8,128)} %copy-done, f32[3072,1]{0,1:T(1,128)S(1)} %bitcast.299), kind=kOutput, calls=%fused_computation.19 | convolution fusion | flops 56623104 | bytes 18892800 | tf_op jit(solution)/shard_map/dot_general | solution.py:68
  571.3 39.9 %psum.98 = f32[12288]{0:T(1024)S(1)} all-reduce(f32[12288]{0:T(1024)S(1)} %dynamic_update_slice.26), channel_id=1, replica_groups=mesh['row'=8,'col'=4] {'row','col'}, use_global_device_ids=true, to_apply=%region_12.13 | all-reduce | flops 12288 | bytes 98304 | tf_op jit(solution)/shard_map/psum | solution.py:72
  612.4 0.7 multiply_subtract_fusion.5
  618.6 1.0 convolution_bitcast_fusion.9
  619.7 1.0 convolution_bitcast_fusion.8
  621.3 12.9 %convolution_reduce_fusion.4 = f32[1536]{0:T(1024)S(1)} fusion(f32[1536,3072]{0,1:T(8,128)} %copy-done, f32[3072,1]{0,1:T(1,128)S(1)} %bitcast.300), kind=kOutput, calls=%fused_computation.18 | convolution fusion | flops 56623104 | bytes 18892800 | tf_op jit(solution)/shard_map/dot_general | solution.py:68
  634.5 41.6 %psum.99 = f32[12288]{0:T(1024)S(1)} all-reduce(f32[12288]{0:T(1024)S(1)} %dynamic_update_slice.27), channel_id=1, replica_groups=mesh['row'=8,'col'=4] {'row','col'}, use_global_device_ids=true, to_apply=%region_15.16 | all-reduce | flops 12288 | bytes 98304 | tf_op jit(solution)/shard_map/psum | solution.py:72
  677.3 0.7 multiply_subtract_fusion.4
  680.4 0.7 fusion.239
  683.8 1.0 convolution_bitcast_fusion.7
  684.8 1.0 convolution_bitcast_fusion.6
  686.5 12.9 %convolution_reduce_fusion.3 = f32[1536]{0:T(1024)S(1)} fusion(f32[1536,3072]{0,1:T(8,128)} %copy-done, f32[3072,1]{0,1:T(1,128)S(1)} %bitcast.301), kind=kOutput, calls=%fused_computation.17 | convolution fusion | flops 56623104 | bytes 18892800 | tf_op jit(solution)/shard_map/dot_general | solution.py:68
  699.7 40.0 %psum.100 = f32[12288]{0:T(1024)S(1)} all-reduce(f32[12288]{0:T(1024)S(1)} %dynamic_update_slice.28), channel_id=1, replica_groups=mesh['row'=8,'col'=4] {'row','col'}, use_global_device_ids=true, to_apply=%region_18.19 | all-reduce | flops 12288 | bytes 98304 | tf_op jit(solution)/shard_map/psum | solution.py:72
  740.9 0.7 multiply_subtract_fusion.3
  742.0 0.6 fusion.215
  744.1 0.6 fusion.238
  747.3 1.0 convolution_bitcast_fusion.5
  748.3 1.0 convolution_bitcast_fusion.4
  749.4 0.7 fusion.232
  750.0 12.9 %convolution_reduce_fusion.2 = f32[1536]{0:T(1024)S(1)} fusion(f32[1536,3072]{0,1:T(8,128)} %copy-done, f32[3072,1]{0,1:T(1,128)S(1)} %bitcast.302), kind=kOutput, calls=%fused_computation.16 | convolution fusion | flops 56623104 | bytes 18892800 | tf_op jit(solution)/shard_map/dot_general | solution.py:68
  763.3 41.2 %psum.101 = f32[12288]{0:T(1024)S(1)} all-reduce(f32[12288]{0:T(1024)S(1)} %dynamic_update_slice.29), channel_id=1, replica_groups=mesh['row'=8,'col'=4] {'row','col'}, use_global_device_ids=true, to_apply=%region_21.22 | all-reduce | flops 12288 | bytes 98304 | tf_op jit(solution)/shard_map/psum | solution.py:72
  805.7 0.7 multiply_subtract_fusion.2
  808.7 0.6 fusion.237
  812.0 1.0 convolution_bitcast_fusion.3
  813.0 1.0 convolution_bitcast_fusion.2
  814.5 12.9 %convolution_reduce_fusion.1 = f32[1536]{0:T(1024)S(1)} fusion(f32[1536,3072]{0,1:T(8,128)} %copy-done, f32[3072,1]{0,1:T(1,128)S(1)} %bitcast.303), kind=kOutput, calls=%fused_computation.15 | convolution fusion | flops 56623104 | bytes 18892800 | tf_op jit(solution)/shard_map/dot_general | solution.py:68
  827.7 40.0 %psum.102 = f32[12288]{0:T(1024)S(1)} all-reduce(f32[12288]{0:T(1024)S(1)} %dynamic_update_slice.30), channel_id=1, replica_groups=mesh['row'=8,'col'=4] {'row','col'}, use_global_device_ids=true, to_apply=%region_24.25 | all-reduce | flops 12288 | bytes 98304 | tf_op jit(solution)/shard_map/psum | solution.py:72
  868.8 0.7 multiply_subtract_fusion.1
  874.8 1.1 convolution_bitcast_fusion.1
  875.9 1.1 convolution_bitcast_fusion
  877.0 18.6 %copy.10 = f32[1536,3072]{1,0:T(8,128)} copy(f32[1536,3072]{0,1:T(8,128)} %copy-done) | data formatting | bytes 37748736
  896.1 12.9 %convolution_reduce_fusion = f32[1536]{0:T(1024)S(1)} fusion(f32[1536,3072]{0,1:T(8,128)} %copy-done, f32[3072,1]{0,1:T(1,128)S(1)} %bitcast.297), kind=kOutput, calls=%fused_computation.14 | convolution fusion | flops 56623104 | bytes 18892800 | tf_op jit(solution)/shard_map/dot_general | solution.py:68
  909.3 41.0 %psum.103 = f32[12288]{0:T(1024)S(1)} all-reduce(f32[12288]{0:T(1024)S(1)} %dynamic_update_slice.31), channel_id=1, replica_groups=mesh['row'=8,'col'=4] {'row','col'}, use_global_device_ids=true, to_apply=%region_27.28 | all-reduce | flops 12288 | bytes 98304 | tf_op jit(solution)/shard_map/psum | solution.py:72
  950.8 0.7 multiply_reduce_fusion
  951.5 0.7 multiply_subtract_fusion
  952.3 5.1 stack.39
  958.1 0.7 fusion.195
  (124 shorter events, 34.3 us)
Async XLA Ops:
  7.2 69.2 %all-gather.5.cloned.1.call-start = ((), (), s32[]{:S(2)}) async-start(), calls=%async_computation.1 | async-start | bytes 3932160 | tf_op jit(solution)/shard_map/all_gather | solution.py:27
  9.9 130.1 %all-gather.3.cloned.1.call-start = ((), (), s32[]{:S(2)}) async-start(), calls=%async_computation | async-start | bytes 3932160 | tf_op jit(solution)/shard_map/all_gather | solution.py:27
  10.6 305.7 %all-reduce.3.cloned.1.call-start = ((), (), s32[]{:S(2)}) async-start(), calls=%async_computation.2 | async-start | bytes 25165824 | tf_op jit(solution)/shard_map/psum | solution.py:13
  146.3 170.1 %copy-start.1 = (f32[1536,512]{1,0:T(8,128)S(1)}, f32[1536,512]{1,0:T(8,128)}, u32[]{:S(2)}) copy-start(f32[1536,512]{1,0:T(8,128)} %all-gather.3.cloned.1.call-done) | copy-start | bytes 9437188
  165.0 185.9 %copy-start.2 = (f32[1536]{0:T(1024)S(1)}, f32[1536]{0:T(1024)}, u32[]{:S(2)}) copy-start(f32[1536]{0:T(1024)} %param.5) | copy-start | bytes 18436
  390.2 6.5 copy-start
Sparse Core Ops, SparseCore 0:
  10.1 66.1 all-gather.4
  77.9 62.0 all-gather.2
  145.7 170.6 all-reduce.2
where the time goes:
time: 974 us; the launch traced here: 966 us
  blocking collectives  352 us (36%)
  waiting for transfers between devices  276 us (28%)
  matrix products  208 us (21%)
  local copies, waits for them, and re-layouts  63.6 us (7%)
  between operations  35.8 us (4%)
  other arithmetic  30 us (3%)
    psum x8, blocking collectives, shards(): image = lax.psum(placed, ('row', 'col'))  323 us
    psum x1, waiting for transfers between devices, from_root(): return lax.psum(jnp.where(mine, value, jnp.zeros_like(value)), axis)  151 us
    all_gather x2, waiting for transfers between devices, shards(): left_rows = lax.all_gather(piece, 'col', axis=0, tiled=True)  124 us
    dot_general x8, matrix products, shards(): partial_rows = jnp.dot(casida, unit_cols, precision=lax.Precision.HIGHEST)  103 us
    dot_general x2, matrix products, shards(): lax.dot_general(left_rows, right_rows, (((1,), (1,)), ((), ())), precisio...  73.9 us
    unnamed x8, local copies, waits for them, and re-layouts  43.9 us
  transfers between devices with their start and end apart: 3, of which 3 were waited for; matrix products, arithmetic and copies ran while one was open for 3% of the time, Pallas kernels for 0%

commit v1 on v0

--- a/solution.py
+++ b/solution.py
@@ -69,7 +69,9 @@
         placed = lax.dynamic_update_slice_in_dim(
             jnp.zeros((total_rows,), jnp.float32), partial_rows, row_index * rows_here, 0
         )
-        image = lax.psum(placed, ("row", "col"))
+        image = placed
+        for dev in ("col", "row"):
+            image = lax.psum(image, axis_name=dev)
         image = image - jnp.dot(
             upper_full,
             jnp.dot(lower_full.T, unit, precision=lax.Precision.HIGHEST),

time: 974 us -> 970 us (level)
    psum x8 -> x16, blocking collectives: 323 us -> 320 us  [shards(): image = lax.psum(image, axis_name=dev)]
where the time goes in v1:
time: 970 us; the launch traced here: 963 us
  blocking collectives  349 us (36%)
  waiting for transfers between devices  276 us (28%)
  matrix products  208 us (21%)
  local copies, waits for them, and re-layouts  63.6 us (7%)
  between operations  35.9 us (4%)
  other arithmetic  30 us (3%)
    psum x16, blocking collectives, shards(): image = lax.psum(image, axis_name=dev)  320 us
    psum x1, waiting for transfers between devices, from_root(): return lax.psum(jnp.where(mine, value, jnp.zeros_like(value)), axis)  151 us
    all_gather x2, waiting for transfers between devices, shards(): left_rows = lax.all_gather(piece, 'col', axis=0, tiled=True)  124 us
    dot_general x8, matrix products, shards(): partial_rows = jnp.dot(casida, unit_cols, precision=lax.Precision.HIGHEST)  103 us
    dot_general x2, matrix products, shards(): lax.dot_general(left_rows, right_rows, (((1,), (1,)), ((), ())), precisio...  73.9 us
    unnamed x8, local copies, waits for them, and re-layouts  43.9 us
    psum x1, blocking collectives, from_root(): return lax.psum(jnp.where(mine, value, jnp.zeros_like(value)), axis)  19.5 us
  transfers between devices with their start and end apart: 3, of which 3 were waited for; matrix products, arithmetic and copies ran while one was open for 3% of the time, Pallas kernels for 0%

profile of v1, /device:TPU:0, one launch (start us, length us, event | category | flops | bytes accessed | tf_op | source)
XLA Modules:
  0.0 962.5 jit_solution(18039939259899225421)
XLA Ops:
  7.2 2.6 fusion.234
  9.9 0.7 all-gather.3.cloned.1.call-update
  10.7 65.6 %all-gather.5.cloned.1.call-done = f32[1536,512]{1,0:T(8,128)} async-done(((f32[384,512]{1,0:T(8,128)}), f32[1536,512]{1,0:T(8,128)}) %all-gather.5.cloned.1.call-update) | async-done | bytes 3145744 | tf_op jit(solution)/shard_map/all_gather | solution.py:27
  76.3 5.6 broadcast_select_fusion.1
  81.9 58.1 %all-gather.3.cloned.1.call-done = f32[1536,512]{1,0:T(8,128)} async-done(((f32[384,512]{1,0:T(8,128)}), f32[1536,512]{1,0:T(8,128)}) %all-gather.3.cloned.1.call-update) | async-done | bytes 3145744 | tf_op jit(solution)/shard_map/all_gather | solution.py:27
  140.0 5.6 broadcast_select_fusion.3
  145.6 0.7 broadcast_reduce_fusion
  146.3 18.8 %copy.9 = f32[1536,3072]{0,1:T(8,128)} copy(f32[1536,3072]{1,0:T(8,128)} %param.4) | data formatting | bytes 37748736 | tf_op args[1]
  165.1 151.2 %all-reduce.3.cloned.1.call-done = (f32[1536,512]{1,0:T(8,128)}, f32[1536,512]{1,0:T(8,128)}, f32[1536,512]{1,0:T(8,128)}, f32[1536,512]{1,0:T(8,128)}) async-done(((f32[1536,512]{1,0:T(8,128)}, f32[1536,512]{1,0:T(8,128)}, f32[1536,512]{1,0:T(8,128)}, f32[1536,512]{1,0:T(8,128)}), (f32[1536,512]{1,0:T(8,128)}, f32[1536,512]{1,0:T(8,128)}, f32[1536,512]{1,0:T(8,128)}, ...) | async-done | bytes 12582928 | tf_op jit(solution)/shard_map/psum | solution.py:13
  316.4 34.6 %fusion.2 = f32[3072,1536]{1,0:T(8,128)} fusion(f32[1536,512]{1,0:T(8,128)S(1)} %copy-done.1, f32[1536,512]{1,0:T(8,128)} %get-tuple-element.12, f32[1536,512]{1,0:T(8,128)} %get-tuple-element.13), kind=kOutput, calls=%fused_computation.3 | convolution fusion | flops 28992602112 | bytes 28311552 | tf_op jit(solution)/shard_map/dot_general | solution.py:32
  351.0 39.2 %fusion.1 = f32[1536,3072]{0,1:T(8,128)S(1)} fusion(f32[1536,3072]{0,1:T(8,128)} %copy.9, f32[3072,1536]{1,0:T(8,128)} %fusion.2, f32[1536,512]{1,0:T(8,128)} %all-gather.5.cloned.1.call-done, f32[1536]{0:T(1024)S(1)} %copy-done.2, s32[1536]{0:T(1024)S(1)} %iota_add_fusion.1, s32[3072]{0:T(1024)S(1)} %iota_add_fusion, f32[1536,512]{1,0:T(8,128)} %get-tuple-element.14, ...), kind=kOutput, calls=%fused_computation.2 | convolution fusion | flops 29020913664 | bytes 66084864 | tf_op jit(solution)/shard_map/dot_general | solution.py:32
  390.2 6.5 copy-done
  396.7 19.5 %psum.151 = f32[1536,8]{0,1:T(8,128)S(1)} all-reduce(f32[1536,8]{0,1:T(8,128)S(1)} %slice_select_fusion), channel_id=1, replica_groups=mesh['row'=8,'col'=4] {'col'}, use_global_device_ids=true, to_apply=%region_4.5 | all-reduce | flops 12288 | bytes 98304 | tf_op jit(solution)/shard_map/psum | solution.py:13
  416.2 9.5 all_gather.11
  426.0 0.7 broadcast.265
  430.6 12.9 %convolution_reduce_fusion.7 = f32[1536]{0:T(1024)S(1)} fusion(f32[1536,3072]{0,1:T(8,128)} %copy-done, f32[3072,1]{0,1:T(1,128)S(1)} %bitcast.304), kind=kOutput, calls=%fused_computation.21 | convolution fusion | flops 56623104 | bytes 18892800 | tf_op jit(solution)/shard_map/dot_general | solution.py:68
  443.8 16.1 %psum.152 = f32[12288]{0:T(1024)S(1)} all-reduce(f32[12288]{0:T(1024)S(1)} %dynamic_update_slice.24), channel_id=1, replica_groups=mesh['row'=8,'col'=4] {'col'}, use_global_device_ids=true, to_apply=%region_6.7 | all-reduce | flops 12288 | bytes 98304 | tf_op jit(solution)/shard_map/psum | solution.py:74
  459.9 22.9 %psum.153 = f32[12288]{0:T(1024)S(1)} all-reduce(f32[12288]{0:T(1024)S(1)} %psum.152), channel_id=1, replica_groups=mesh['row'=8,'col'=4] {'row'}, use_global_device_ids=true, to_apply=%region_7.8 | all-reduce | flops 12288 | bytes 98304 | tf_op jit(solution)/shard_map/psum | solution.py:74
  482.8 1.6 fusion.12
  484.4 0.7 broadcast.267
  491.8 1.0 convolution_bitcast_fusion.13
  492.8 1.0 convolution_bitcast_fusion.12
  494.4 12.9 %convolution_reduce_fusion.6 = f32[1536]{0:T(1024)S(1)} fusion(f32[1536,3072]{0,1:T(8,128)} %copy-done, f32[3072,1]{0,1:T(1,128)S(1)} %bitcast.298), kind=kOutput, calls=%fused_computation.20 | convolution fusion | flops 56623104 | bytes 18892800 | tf_op jit(solution)/shard_map/dot_general | solution.py:68
  507.6 17.9 %psum.154 = f32[12288]{0:T(1024)S(1)} all-reduce(f32[12288]{0:T(1024)S(1)} %dynamic_update_slice.25), channel_id=1, replica_groups=mesh['row'=8,'col'=4] {'col'}, use_global_device_ids=true, to_apply=%region_10.11 | all-reduce | flops 12288 | bytes 98304 | tf_op jit(solution)/shard_map/psum | solution.py:74
  525.5 23.0 %psum.155 = f32[12288]{0:T(1024)S(1)} all-reduce(f32[12288]{0:T(1024)S(1)} %psum.154), channel_id=1, replica_groups=mesh['row'=8,'col'=4] {'row'}, use_global_device_ids=true, to_apply=%region_11.12 | all-reduce | flops 12288 | bytes 98304 | tf_op jit(solution)/shard_map/psum | solution.py:74
  549.7 0.7 multiply_subtract_fusion.6
  555.9 1.0 convolution_bitcast_fusion.11
  556.9 1.0 convolution_bitcast_fusion.10
  558.5 12.9 %convolution_reduce_fusion.5 = f32[1536]{0:T(1024)S(1)} fusion(f32[1536,3072]{0,1:T(8,128)} %copy-done, f32[3072,1]{0,1:T(1,128)S(1)} %bitcast.299), kind=kOutput, calls=%fused_computation.19 | convolution fusion | flops 56623104 | bytes 18892800 | tf_op jit(solution)/shard_map/dot_general | solution.py:68
  571.7 16.1 %psum.156 = f32[12288]{0:T(1024)S(1)} all-reduce(f32[12288]{0:T(1024)S(1)} %dynamic_update_slice.26), channel_id=1, replica_groups=mesh['row'=8,'col'=4] {'col'}, use_global_device_ids=true, to_apply=%region_14.15 | all-reduce | flops 12288 | bytes 98304 | tf_op jit(solution)/shard_map/psum | solution.py:74
  587.9 23.0 %psum.157 = f32[12288]{0:T(1024)S(1)} all-reduce(f32[12288]{0:T(1024)S(1)} %psum.156), channel_id=1, replica_groups=mesh['row'=8,'col'=4] {'row'}, use_global_device_ids=true, to_apply=%region_15.16 | all-reduce | flops 12288 | bytes 98304 | tf_op jit(solution)/shard_map/psum | solution.py:74
  612.1 0.7 multiply_subtract_fusion.5
  618.4 1.0 convolution_bitcast_fusion.9
  619.4 1.0 convolution_bitcast_fusion.8
  621.1 12.9 %convolution_reduce_fusion.4 = f32[1536]{0:T(1024)S(1)} fusion(f32[1536,3072]{0,1:T(8,128)} %copy-done, f32[3072,1]{0,1:T(1,128)S(1)} %bitcast.300), kind=kOutput, calls=%fused_computation.18 | convolution fusion | flops 56623104 | bytes 18892800 | tf_op jit(solution)/shard_map/dot_general | solution.py:68
  634.3 17.8 %psum.158 = f32[12288]{0:T(1024)S(1)} all-reduce(f32[12288]{0:T(1024)S(1)} %dynamic_update_slice.27), channel_id=1, replica_groups=mesh['row'=8,'col'=4] {'col'}, use_global_device_ids=true, to_apply=%region_18.19 | all-reduce | flops 12288 | bytes 98304 | tf_op jit(solution)/shard_map/psum | solution.py:74
  652.1 23.3 %psum.159 = f32[12288]{0:T(1024)S(1)} all-reduce(f32[12288]{0:T(1024)S(1)} %psum.158), channel_id=1, replica_groups=mesh['row'=8,'col'=4] {'row'}, use_global_device_ids=true, to_apply=%region_19.20 | all-reduce | flops 12288 | bytes 98304 | tf_op jit(solution)/shard_map/psum | solution.py:74
  676.6 0.7 multiply_subtract_fusion.4
  679.7 0.7 fusion.239
  683.1 1.0 convolution_bitcast_fusion.7
  684.1 1.0 convolution_bitcast_fusion.6
  685.8 12.9 %convolution_reduce_fusion.3 = f32[1536]{0:T(1024)S(1)} fusion(f32[1536,3072]{0,1:T(8,128)} %copy-done, f32[3072,1]{0,1:T(1,128)S(1)} %bitcast.301), kind=kOutput, calls=%fused_computation.17 | convolution fusion | flops 56623104 | bytes 18892800 | tf_op jit(solution)/shard_map/dot_general | solution.py:68
  699.0 16.2 %psum.160 = f32[12288]{0:T(1024)S(1)} all-reduce(f32[12288]{0:T(1024)S(1)} %dynamic_update_slice.28), channel_id=1, replica_groups=mesh['row'=8,'col'=4] {'col'}, use_global_device_ids=true, to_apply=%region_22.23 | all-reduce | flops 12288 | bytes 98304 | tf_op jit(solution)/shard_map/psum | solution.py:74
  715.2 23.0 %psum.161 = f32[12288]{0:T(1024)S(1)} all-reduce(f32[12288]{0:T(1024)S(1)} %psum.160), channel_id=1, replica_groups=mesh['row'=8,'col'=4] {'row'}, use_global_device_ids=true, to_apply=%region_23.24 | all-reduce | flops 12288 | bytes 98304 | tf_op jit(solution)/shard_map/psum | solution.py:74
  745.8 1.0 convolution_bitcast_fusion.5
  746.8 1.0 convolution_bitcast_fusion.4
  748.5 12.9 %convolution_reduce_fusion.2 = f32[1536]{0:T(1024)S(1)} fusion(f32[1536,3072]{0,1:T(8,128)} %copy-done, f32[3072,1]{0,1:T(1,128)S(1)} %bitcast.302), kind=kOutput, calls=%fused_computation.16 | convolution fusion | flops 56623104 | bytes 18892800 | tf_op jit(solution)/shard_map/dot_general | solution.py:68
  761.7 17.8 %psum.162 = f32[12288]{0:T(1024)S(1)} all-reduce(f32[12288]{0:T(1024)S(1)} %dynamic_update_slice.29), channel_id=1, replica_groups=mesh['row'=8,'col'=4] {'col'}, use_global_device_ids=true, to_apply=%region_26.27 | all-reduce | flops 12288 | bytes 98304 | tf_op jit(solution)/shard_map/psum | solution.py:74
  779.6 23.0 %psum.163 = f32[12288]{0:T(1024)S(1)} all-reduce(f32[12288]{0:T(1024)S(1)} %psum.162), channel_id=1, replica_groups=mesh['row'=8,'col'=4] {'row'}, use_global_device_ids=true, to_apply=%region_27.28 | all-reduce | flops 12288 | bytes 98304 | tf_op jit(solution)/shard_map/psum | solution.py:74
  810.1 1.0 convolution_bitcast_fusion.3
  811.1 1.0 convolution_bitcast_fusion.2
  812.6 12.9 %convolution_reduce_fusion.1 = f32[1536]{0:T(1024)S(1)} fusion(f32[1536,3072]{0,1:T(8,128)} %copy-done, f32[3072,1]{0,1:T(1,128)S(1)} %bitcast.303), kind=kOutput, calls=%fused_computation.15 | convolution fusion | flops 56623104 | bytes 18892800 | tf_op jit(solution)/shard_map/dot_general | solution.py:68
  825.8 16.3 %psum.164 = f32[12288]{0:T(1024)S(1)} all-reduce(f32[12288]{0:T(1024)S(1)} %dynamic_update_slice.30), channel_id=1, replica_groups=mesh['row'=8,'col'=4] {'col'}, use_global_device_ids=true, to_apply=%region_30.31 | all-reduce | flops 12288 | bytes 98304 | tf_op jit(solution)/shard_map/psum | solution.py:74
  842.1 23.0 %psum.165 = f32[12288]{0:T(1024)S(1)} all-reduce(f32[12288]{0:T(1024)S(1)} %psum.164), channel_id=1, replica_groups=mesh['row'=8,'col'=4] {'row'}, use_global_device_ids=true, to_apply=%region_31.32 | all-reduce | flops 12288 | bytes 98304 | tf_op jit(solution)/shard_map/psum | solution.py:74
  872.3 1.1 convolution_bitcast_fusion.1
  873.3 1.1 convolution_bitcast_fusion
  874.5 18.6 %copy.10 = f32[1536,3072]{1,0:T(8,128)} copy(f32[1536,3072]{0,1:T(8,128)} %copy-done) | data formatting | bytes 37748736
  893.6 12.9 %convolution_reduce_fusion = f32[1536]{0:T(1024)S(1)} fusion(f32[1536,3072]{0,1:T(8,128)} %copy-done, f32[3072,1]{0,1:T(1,128)S(1)} %bitcast.297), kind=kOutput, calls=%fused_computation.14 | convolution fusion | flops 56623104 | bytes 18892800 | tf_op jit(solution)/shard_map/dot_general | solution.py:68
  906.8 17.7 %psum.166 = f32[12288]{0:T(1024)S(1)} all-reduce(f32[12288]{0:T(1024)S(1)} %dynamic_update_slice.31), channel_id=1, replica_groups=mesh['row'=8,'col'=4] {'col'}, use_global_device_ids=true, to_apply=%region_34.35 | all-reduce | flops 12288 | bytes 98304 | tf_op jit(solution)/shard_map/psum | solution.py:74
  924.5 22.8 %psum.167 = f32[12288]{0:T(1024)S(1)} all-reduce(f32[12288]{0:T(1024)S(1)} %psum.166), channel_id=1, replica_groups=mesh['row'=8,'col'=4] {'row'}, use_global_device_ids=true, to_apply=%region_35.36 | all-reduce | flops 12288 | bytes 98304 | tf_op jit(solution)/shard_map/psum | solution.py:74
  947.8 0.7 multiply_reduce_fusion
  948.5 0.7 multiply_subtract_fusion
  949.3 5.1 stack.39
  955.0 0.7 fusion.195
  (132 shorter events, 39.5 us)
Async XLA Ops:
  7.2 69.2 %all-gather.5.cloned.1.call-start = ((), (), s32[]{:S(2)}) async-start(), calls=%async_computation.1 | async-start | bytes 3932160 | tf_op jit(solution)/shard_map/all_gather | solution.py:27
  9.9 130.1 %all-gather.3.cloned.1.call-start = ((), (), s32[]{:S(2)}) async-start(), calls=%async_computation | async-start | bytes 3932160 | tf_op jit(solution)/shard_map/all_gather | solution.py:27
  10.6 305.7 %all-reduce.3.cloned.1.call-start = ((), (), s32[]{:S(2)}) async-start(), calls=%async_computation.2 | async-start | bytes 25165824 | tf_op jit(solution)/shard_map/psum | solution.py:13
  146.3 170.1 %copy-start.1 = (f32[1536,512]{1,0:T(8,128)S(1)}, f32[1536,512]{1,0:T(8,128)}, u32[]{:S(2)}) copy-start(f32[1536,512]{1,0:T(8,128)} %all-gather.3.cloned.1.call-done) | copy-start | bytes 9437188
  165.0 185.9 %copy-start.2 = (f32[1536]{0:T(1024)S(1)}, f32[1536]{0:T(1024)}, u32[]{:S(2)}) copy-start(f32[1536]{0:T(1024)} %param.5) | copy-start | bytes 18436
  390.2 6.5 copy-start
Sparse Core Ops, SparseCore 0:
  10.1 66.1 all-gather.4
  77.9 62.0 all-gather.2
  145.7 170.6 all-reduce.2
